TPU v7x, 256 devices: a whole 4x4x8 slice. The times are simulated.
256 devices in a mesh: dp: 32 (over z, x_hi, core), tensor: 8 (over y, x_lo).
Axes of the slice: x: 4 (x_hi: 2, x_lo: 2; x = x_hi * 2 + x_lo), y: 4, z: 8, core: 2. Of those that a mesh axis runs over, the one named last changes fastest.
Arguments:
- hidden_in: bfloat16 [12288, 4096], P('dp'), may hold values from -6 to 6
- upstream: bfloat16 [12288, 4096], P('dp'), may hold values from -6 to 6
- merged_input_weight: bfloat16 [4096, 6144], P('dp', 'tensor'), may hold values from -0.09375 to 0.09375
- output_matrix: bfloat16 [4096, 4096], P('dp', 'tensor'), may hold values from -0.09375 to 0.09375
- norm_gain: float32 [4096], replicated, may hold values from 0.5 to 1.5
- query_gain: float32 [128], replicated, may hold values from 0.5 to 1.5
- key_gain: float32 [128], replicated, may hold values from 0.5 to 1.5
Outputs:
- hidden_grad: bfloat16 [12288, 4096], P('dp')
- input_grad: float32 [4096, 6144], P('dp', 'tensor')
- output_grad: float32 [4096, 4096], P('dp', 'tensor')
- gain_grad: float32 [4096], replicated
- query_grad: float32 [128], replicated
- key_grad: float32 [128], replicated
All inputs are finite; a program needn't handle non-finite values.
Results may differ from a plain program's by a relative error of at most 0.015.
Values may be sent and summed in bfloat16 or wider, within the bound.
No kernel may reach another device: no remote copies, remote signals or barrier semaphores. Data moves between devices by JAX's collectives and lax.ppermute only.
A program may use at most 128 MiB of HBM per device.

v0:
```python
from functools import partial
import functools
import math
import jax
import jax.numpy as jnp
from jax import lax
from jax.sharding import Mesh
from jax.sharding import PartitionSpec as P

QUERY_HEADS = 32
KEY_VALUE_HEADS = 8
HEAD_SIZE = 128
TENSOR = ("tensor_0", "tensor_1")
DP = ("dp_0", "dp_1", "dp_2")
DP_TENSOR = ("dp_0", "dp_1", "dp_2", "tensor_0", "tensor_1")
EPSILON = 1e-06
ROPE_BASE = 1000000.0


def sent_to_all(x, axis):
    peers = lax.axis_size(axis)
    return lax.all_to_all(jnp.broadcast_to(x[None], (peers, *x.shape)), axis, 0, 0, tiled=True)


def joined_along(tiles, dim):
    lengths = list(tiles.shape[1:])
    lengths[dim] *= tiles.shape[0]
    return jnp.moveaxis(tiles, 0, dim).reshape(lengths)


def gathered_by_axis(x, axes, dim):
    far, near = axes
    tiles = sent_to_all(sent_to_all(x, far), near)
    return joined_along(tiles.swapaxes(0, 1).reshape(-1, *x.shape), dim)


def collect(x, axis, dim):
    tiles = sent_to_all(x, axis)
    return joined_along(tiles, dim)


def by_axis(x, axes):
    return functools.reduce(lax.psum, axes, x)


def norm_rows(states, scaling):
    inverse = lax.rsqrt(jnp.mean(states * states, axis=-1, keepdims=True) + EPSILON)
    return states * inverse * scaling


def rope_tables(length, columns):
    half_width = columns // 2
    exponent = jnp.arange(half_width, dtype=jnp.float32) * (2.0 / columns)
    frequency = jnp.exp(-exponent * math.log(ROPE_BASE))
    places = jnp.arange(length, dtype=jnp.float32)
    angles = places[:, None] * frequency[None, :]
    return (jnp.cos(angles), jnp.sin(angles))


def head_post(projected_rows, scaling, cosine, sine):
    inverse = lax.rsqrt(jnp.mean(projected_rows * projected_rows, axis=-1, keepdims=True) + EPSILON)
    normed = projected_rows * inverse * scaling
    half_width = projected_rows.shape[-1] // 2
    layout = (projected_rows.shape[0],) + (1,) * (projected_rows.ndim - 2) + (half_width,)
    cosine_part = cosine.reshape(layout)
    sine_part = sine.reshape(layout)
    leading = normed[..., :half_width]
    trailing = normed[..., half_width:]
    return jnp.concatenate(
        [
            leading * cosine_part - trailing * sine_part,
            trailing * cosine_part + leading * sine_part,
        ],
        axis=-1,
    )


def attend_forward(queries, keys, value_rows, score_scale):
    length = queries.shape[0]
    scores = (
        jnp.einsum("tkgh,skh->kgts", queries, keys, preferred_element_type=jnp.float32)
        * score_scale
    )
    causal = lax.broadcasted_iota(jnp.int32, (length, length), 0) >= lax.broadcasted_iota(
        jnp.int32, (length, length), 1
    )
    raised = jnp.where(causal, jnp.exp(scores), 0.0)
    softmax = raised / jnp.sum(raised, axis=-1, keepdims=True)
    softmax_low = softmax.astype(jnp.bfloat16)
    context = jnp.einsum(
        "kgts,skh->tkgh", softmax_low, value_rows, preferred_element_type=jnp.float32
    )
    return (softmax, softmax_low, context)


def attend_backward(queries, keys, value_rows, softmax, softmax_low, context_gradient, score_scale):
    grad_probs = jnp.einsum(
        "tkgh,skh->kgts", context_gradient, value_rows, preferred_element_type=jnp.float32
    )
    centre = jnp.sum(softmax * grad_probs, axis=-1, keepdims=True)
    grad_scores = (softmax * (grad_probs - centre) * score_scale).astype(jnp.bfloat16)
    grad_values = jnp.einsum(
        "kgts,tkgh->skh", softmax_low, context_gradient, preferred_element_type=jnp.float32
    )
    grad_queries = jnp.einsum(
        "kgts,skh->tkgh", grad_scores, keys, preferred_element_type=jnp.float32
    )
    grad_keys = jnp.einsum(
        "kgts,tkgh->skh", grad_scores, queries, preferred_element_type=jnp.float32
    )
    return (grad_queries, grad_keys, grad_values)


def local(hidden_in, upstream, merged_input_weight, output_matrix, norm_gain, query_gain, key_gain):
    shard_ranks = lax.axis_size(TENSOR)
    groups = lax.axis_size(DP)
    query_heads = QUERY_HEADS // shard_ranks
    key_head_rows = KEY_VALUE_HEADS // shard_ranks
    group_width = QUERY_HEADS // KEY_VALUE_HEADS
    query_columns = query_heads * HEAD_SIZE
    key_columns = key_head_rows * HEAD_SIZE
    score_scale = 1.0 / math.sqrt(HEAD_SIZE)
    length = hidden_in.shape[0]
    share = length // shard_ranks
    share_start = lax.axis_index(TENSOR) * share
    grad_scale = 1.0 / math.sqrt(groups * length)
    local_norm, norm_back = jax.vjp(norm_rows, hidden_in.astype(jnp.float32), norm_gain)
    normed = local_norm.astype(jnp.bfloat16)
    full_weight = lax.all_gather(merged_input_weight, DP, axis=0, tiled=True)
    projected_rows = jnp.dot(normed, full_weight, preferred_element_type=jnp.float32)
    unnormed_query = projected_rows[:, :query_columns].reshape(
        length, key_head_rows, group_width, HEAD_SIZE
    )
    unnormed_key = projected_rows[:, query_columns : query_columns + key_columns].reshape(
        length, key_head_rows, HEAD_SIZE
    )
    value_rows = (
        projected_rows[:, query_columns + key_columns :]
        .astype(jnp.bfloat16)
        .reshape(length, key_head_rows, HEAD_SIZE)
    )
    cosine, sine = rope_tables(length, HEAD_SIZE)
    post = partial(head_post, cosine=cosine, sine=sine)
    queries_full, query_back = jax.vjp(post, unnormed_query, query_gain)
    keys_full, key_back = jax.vjp(post, unnormed_key, key_gain)
    queries = queries_full.astype(jnp.bfloat16)
    keys = keys_full.astype(jnp.bfloat16)
    context_gradient = jnp.dot(
        upstream,
        gathered_by_axis(output_matrix, (("dp_0", "dp_1"), "dp_2"), 0),
        preferred_element_type=jnp.float32,
    )
    context_gradient = context_gradient.astype(jnp.bfloat16).reshape(
        length, key_head_rows, group_width, HEAD_SIZE
    )
    softmax, softmax_low, context = attend_forward(queries, keys, value_rows, score_scale)
    context_low = context.astype(jnp.bfloat16).reshape(length, query_columns)
    grad_queries, grad_keys, grad_values = attend_backward(
        queries, keys, value_rows, softmax, softmax_low, context_gradient, score_scale
    )
    grad_raw_query, query_part = query_back(grad_queries)
    grad_raw_key, key_part = key_back(grad_keys)
    grad_projected = jnp.concatenate(
        [
            grad_raw_query.reshape(length, query_columns),
            grad_raw_key.reshape(length, key_columns),
            grad_values.reshape(length, key_columns),
        ],
        axis=1,
    ).astype(jnp.bfloat16)
    own_hidden = lax.dynamic_slice_in_dim(hidden_in, share_start, share, 0).astype(jnp.float32)
    own_upstream = lax.dynamic_slice_in_dim(upstream, share_start, share, 0).astype(jnp.float32)
    rows = grad_projected
    grad_share = lax.psum_scatter(
        lax.dot_general(
            rows, full_weight, (((1,), (1,)), ((), ())), preferred_element_type=jnp.float32
        ).astype(jnp.bfloat16),
        TENSOR,
        scatter_dimension=0,
        tiled=True,
    ).astype(jnp.float32)
    share_norm, share_back = jax.vjp(norm_rows, own_hidden, norm_gain)
    grad_own, gain_part = share_back(grad_share)
    own_rows = (own_upstream + grad_own).astype(jnp.bfloat16)
    hidden_grad = collect(own_rows, TENSOR, 0)
    rows = upstream
    joined = lax.psum_scatter(
        jnp.concatenate(
            [
                lax.dot_general(
                    normed,
                    grad_projected,
                    (((0,), (0,)), ((), ())),
                    preferred_element_type=jnp.float32,
                )
                * grad_scale,
                lax.dot_general(
                    rows, context_low, (((0,), (0,)), ((), ())), preferred_element_type=jnp.float32
                )
                * grad_scale,
            ],
            axis=1,
        ).astype(jnp.bfloat16),
        DP,
        scatter_dimension=0,
        tiled=True,
    ).astype(jnp.float32)
    input_grad = joined[:, : merged_input_weight.shape[1]]
    output_grad = joined[:, merged_input_weight.shape[1] :]
    gain_sum, query_sum, key_sum = (
        by_axis(gain_part, DP_TENSOR),
        by_axis(query_part, DP_TENSOR),
        by_axis(key_part, DP_TENSOR),
    )
    return (
        hidden_grad,
        input_grad,
        output_grad,
        gain_sum * grad_scale,
        query_sum * grad_scale,
        key_sum * grad_scale,
    )


def solution(mesh):
    split = Mesh(
        mesh.devices.reshape(8, 2, 2, 4, 2), ("dp_0", "dp_1", "dp_2", "tensor_0", "tensor_1")
    )
    return jax.shard_map(
        local,
        mesh=split,
        in_specs=(P(DP, None), P(DP, None), P(DP, TENSOR), P(DP, TENSOR), P(), P(), P()),
        out_specs=(P(DP, None), P(DP, TENSOR), P(DP, TENSOR), P(), P(), P()),
        check_vma=False,
    )
```

profile of v0, /device:TPU:16, one launch (start us, length us, event | category | flops | bytes accessed | tf_op | source)
XLA Modules:
  0.0 413.0 jit_solution(11198640419863443358)
XLA Ops:
  7.9 2.4 broadcast_in_dim.22
  10.3 11.0 %all-to-all-start = ((bf16[16,128,512]{2,1,0:T(8,128)(2,1)}), bf16[16,128,512]{2,1,0:T(8,128)(2,1)S(1)}, u32[]{:S(2)}, u32[]{:S(2)}) async-start(bf16[16,128,512]{2,1,0:T(8,128)(2,1)} %broadcast_in_dim.22), calls=%async_computation | async-start | bytes 4194304 | tf_op jit(solution)/shard_map/all_to_all | solution.py:22
  22.1 2.6 fusion
  26.1 54.7 %all-to-all-done = bf16[16,128,512]{2,1,0:T(8,128)(2,1)S(1)} async-done(((bf16[16,128,512]{2,1,0:T(8,128)(2,1)}), bf16[16,128,512]{2,1,0:T(8,128)(2,1)S(1)}, u32[]{:S(2)}, u32[]{:S(2)}) %all-to-all-start) | async-done | bytes 2097184 | tf_op jit(solution)/shard_map/all_to_all | solution.py:22
  81.3 7.1 %all_to_all.15 = bf16[2,16,128,512]{3,2,1,0:T(8,128)(2,1)S(1)} all-to-all(bf16[2,16,128,512]{3,2,1,0:T(8,128)(2,1)S(1)} %broadcast_in_dim.23), channel_id=1, replica_groups=mesh['dp_0'=8,'dp_1'=2,'dp_2'=2,'tensor_0'=4,'tensor_1'=2] {'dp_2'}, dimensions={0} | all-to-all | bytes 8388608 | tf_op jit(solution)/shard_map/all_to_all | solution.py:22
  90.3 2.5 convolution_convert_fusion.2
  92.8 1.9 copy.126
  94.7 32.5 %all-gather.2.cloned.1.call-done = bf16[4096,768]{1,0:T(8,128)(2,1)} async-done(((bf16[128,768]{1,0:T(8,128)(2,1)}), bf16[4096,768]{1,0:T(8,128)(2,1)}) %all-gather.2.cloned.1.call-update) | async-done | bytes 6291472 | tf_op jit(solution)/shard_map/all_gather | solution.py:129
  127.2 5.4 %fusion.26 = f32[384,768]{1,0:T(8,128)S(1)} fusion(bf16[4096,768]{1,0:T(8,128)(2,1)} %all-gather.2.cloned.1.call-done, bf16[384,4096]{1,0:T(8,128)(2,1)S(1)} %copy-done, f32[4096]{0:T(1024)S(1)} %copy-done.10, f32[384]{0:T(512)} %add_rsqrt_fusion), kind=kOutput, calls=%fused_computation.40 | convolution fusion | flops 2422210560 | bytes 10634752 | tf_op jit(solution)/shard_map/dot_general | solution.py:130
  151.2 7.1 %convolution_convert_fusion = bf16[384,4096]{1,0:T(8,128)(2,1)} fusion(bf16[4096,768]{1,0:T(8,128)(2,1)} %all-gather.2.cloned.1.call-done, bf16[384,128]{0,1:T(8,128)(2,1)S(1)} %copy-done.29, bf16[384,128]{0,1:T(8,128)(2,1)S(1)} %copy.107, bf16[384,512]{0,1:T(8,128)(2,1)S(1)} %bitcast.135), kind=kOutput, calls=%fused_computation.8 | convolution fusion | flops 2419261440 | bytes 10027008 | tf_op jit(solution)/shard_map/dot_general | solution.py:175
  159.2 1.9 convolution_convert_fusion.1
  161.2 2.3 fusion.3
  163.6 3.9 multiply_convert_fusion
  167.5 9.6 %pad_maximum_fusion = bf16[4096,1280]{0,1:T(8,128)(2,1)} fusion(bf16[4096,512]{0,1:T(8,128)(2,1)S(1)} %fusion.3, bf16[4096,768]{0,1:T(8,128)(2,1)S(1)} %multiply_convert_fusion), kind=kLoop, calls=%fused_computation.1 | loop fusion | flops 20971520 | bytes 20971520 | tf_op jit(solution)/shard_map/concatenate | solution.py:188
  177.0 14.4 %copy.124 = bf16[4096,1280]{1,0:T(8,128)(2,1)} copy(bf16[4096,1280]{0,1:T(8,128)(2,1)} %pad_maximum_fusion) | data formatting | bytes 20971520
  191.7 36.7 %reduce-scatter.5.cloned.1.call-done = bf16[48,4096]{1,0:T(8,128)(2,1)} async-done(((bf16[384,4096]{1,0:T(8,128)(2,1)}), bf16[48,4096]{1,0:T(8,128)(2,1)}) %reduce-scatter.5.cloned.1.call-update) | async-done | bytes 393232 | tf_op jit(solution)/shard_map/reduce_scatter | solution.py:174
  231.2 2.0 broadcast_in_dim.27
  233.2 5.6 %all-to-all-start.2 = ((bf16[8,48,4096]{2,1,0:T(8,128)(2,1)}), bf16[8,48,4096]{2,1,0:T(8,128)(2,1)S(1)}, u32[]{:S(2)}, u32[]{:S(2)}) async-start(bf16[8,48,4096]{2,1,0:T(8,128)(2,1)} %broadcast_in_dim.27), calls=%async_computation.3 | async-start | bytes 6291456 | tf_op jit(solution)/shard_map/all_to_all | solution.py:22
  238.8 30.2 %all-reduce.4 = (f32[4096]{0:T(1024)S(1)}, f32[128]{0:T(128)S(1)}, f32[128]{0:T(128)S(1)}) all-reduce(f32[4096]{0:T(1024)S(1)} %get-tuple-element.36, f32[128]{0:T(128)S(1)} %get-tuple-element.38, f32[128]{0:T(128)S(1)} %get-tuple-element.40), channel_id=1, replica_groups=mesh['dp_0'=8,'dp_1'=2,'dp_2'=2,'tensor_0'=4,'tensor_1'=2] {'dp_0'}, use_global_device_ids=true, to_apply=%region_12.13 | all-reduce | flops 4352 | bytes 34816 | tf_op jit(solution)/shard_map/psum | solution.py:43
  269.0 11.1 %all-reduce.8 = (f32[4096]{0:T(1024)S(1)}, f32[128]{0:T(128)S(1)}, f32[128]{0:T(128)S(1)}) all-reduce(f32[4096]{0:T(1024)S(1)} %get-tuple-element.42, f32[128]{0:T(128)S(1)} %get-tuple-element.43, f32[128]{0:T(128)S(1)} %get-tuple-element.44), channel_id=1, replica_groups=mesh['dp_0'=8,'dp_1'=2,'dp_2'=2,'tensor_0'=4,'tensor_1'=2] {'dp_1'}, use_global_device_ids=true, to_apply=%region_13.14 | all-reduce | flops 4352 | bytes 34816 | tf_op jit(solution)/shard_map/psum | solution.py:43
  280.1 3.4 all-reduce.7
  283.5 15.4 %all-reduce.5 = (f32[4096]{0:T(1024)S(1)}, f32[128]{0:T(128)S(1)}, f32[128]{0:T(128)S(1)}) all-reduce(f32[4096]{0:T(1024)S(1)} %get-tuple-element.51, f32[128]{0:T(128)S(1)} %get-tuple-element.52, f32[128]{0:T(128)S(1)} %get-tuple-element.53), channel_id=1, replica_groups=mesh['dp_0'=8,'dp_1'=2,'dp_2'=2,'tensor_0'=4,'tensor_1'=2] {'tensor_0'}, use_global_device_ids=true, to_apply=%region_15.16 | all-reduce | flops 4352 | bytes 34816 | tf_op jit(solution)/shard_map/psum | solution.py:43
  299.0 8.0 %all-reduce.6 = (f32[4096]{0:T(1024)S(1)}, f32[128]{0:T(128)S(1)}, f32[128]{0:T(128)S(1)}) all-reduce(f32[4096]{0:T(1024)S(1)} %get-tuple-element.45, f32[128]{0:T(128)S(1)} %get-tuple-element.46, f32[128]{0:T(128)S(1)} %get-tuple-element.47), channel_id=1, replica_groups=mesh['dp_0'=8,'dp_1'=2,'dp_2'=2,'tensor_0'=4,'tensor_1'=2] {'tensor_1'}, use_global_device_ids=true, to_apply=%region_16.17 | all-reduce | flops 4352 | bytes 34816 | tf_op jit(solution)/shard_map/psum | solution.py:43
  308.1 89.4 %reduce-scatter.7.cloned.1.call-done = bf16[128,1280]{1,0:T(8,128)(2,1)} async-done(((bf16[4096,1280]{1,0:T(8,128)(2,1)}), bf16[128,1280]{1,0:T(8,128)(2,1)}) %reduce-scatter.7.cloned.1.call-update) | async-done | bytes 327696
  (114 shorter events, 37.5 us)
Async XLA Ops:
  7.2 120.1 %all-gather.2.cloned.1.call-start = ((), (), s32[]{:S(2)}) async-start(), calls=%async_computation.5 | async-start | bytes 6488064 | tf_op jit(solution)/shard_map/all_gather | solution.py:129
  10.3 70.4 %all-to-all-start = ((bf16[16,128,512]{2,1,0:T(8,128)(2,1)}), bf16[16,128,512]{2,1,0:T(8,128)(2,1)S(1)}, u32[]{:S(2)}, u32[]{:S(2)}) async-start(bf16[16,128,512]{2,1,0:T(8,128)(2,1)} %broadcast_in_dim.22), calls=%async_computation | async-start | bytes 4194304 | tf_op jit(solution)/shard_map/all_to_all | solution.py:22
  21.4 207.0 %reduce-scatter.5.cloned.1.call-start = ((), (), s32[]{:S(2)}) async-start(), calls=%async_computation.6 | async-start | bytes 3538944 | tf_op jit(solution)/shard_map/reduce_scatter | solution.py:174
  21.4 59.8 %copy-start.25 = (f32[64]{0:T(128)}, f32[64]{0:T(128)S(1)}, u32[]{:S(2)}) copy-start(f32[64]{0:T(128)S(1)} %multiply_exponential_fusion) | copy-start | bytes 772
  26.0 110.9 %copy-start.3 = (f32[384,64]{1,0:T(8,128)}, f32[384,64]{1,0:T(8,128)S(1)}, u32[]{:S(2)}) copy-start(f32[384,64]{1,0:T(8,128)S(1)} %get-tuple-element.66) | copy-start | bytes 294916
  90.3 37.0 %copy-start = (bf16[384,4096]{1,0:T(8,128)(2,1)S(1)}, bf16[384,4096]{1,0:T(8,128)(2,1)}, u32[]{:S(2)}) copy-start(bf16[384,4096]{1,0:T(8,128)(2,1)} %param.7) | copy-start | bytes 9437188
  90.3 37.0 %copy-start.10 = (f32[4096]{0:T(1024)S(1)}, f32[4096]{0:T(1024)}, u32[]{:S(2)}) copy-start(f32[4096]{0:T(1024)} %param.11) | copy-start | bytes 49156
  132.7 3.1 copy-start.26
  133.7 2.9 copy-start.21
  133.9 3.1 copy-start.17
  134.7 2.6 copy-start.11
  134.8 2.6 copy-start.15
  138.3 3.8 copy-start.19
  144.9 2.7 copy-start.27
  144.9 3.8 copy-start.16
  144.9 3.8 copy-start.24
  145.0 4.9 %copy-start.18 = (f32[384]{0:T(512)S(1)}, f32[384]{0:T(512)}, u32[]{:S(2)}) copy-start(f32[384]{0:T(512)} %copy-done.17) | copy-start | bytes 4612
  145.0 6.2 %copy-start.29 = (bf16[384,128]{0,1:T(8,128)(2,1)S(1)}, bf16[384,128]{0,1:T(8,128)(2,1)}, u32[]{:S(2)}) copy-start(bf16[384,128]{0,1:T(8,128)(2,1)} %fusion.20) | copy-start | bytes 294916
  147.6 3.5 copy-start.8
  158.3 239.1 %reduce-scatter.7.cloned.1.call-start = ((), (), s32[]{:S(2)}) async-start(), calls=%async_computation.7 | async-start | bytes 10813440
  161.2 2.4 copy-start.1
  161.2 2.4 copy-start.9
  161.2 2.4 copy-start.28
  233.2 74.8 %all-to-all-start.2 = ((bf16[8,48,4096]{2,1,0:T(8,128)(2,1)}), bf16[8,48,4096]{2,1,0:T(8,128)(2,1)S(1)}, u32[]{:S(2)}, u32[]{:S(2)}) async-start(bf16[8,48,4096]{2,1,0:T(8,128)(2,1)} %broadcast_in_dim.27), calls=%async_computation.3 | async-start | bytes 6291456 | tf_op jit(solution)/shard_map/all_to_all | solution.py:22
  (11 other events, 14.9 us)
Sparse Core Ops, SparseCore 0:
  10.7 116.4 all-gather.1
  158.5 69.8 reduce-scatter.4
  232.8 164.6 reduce-scatter.6
where the time goes:
time: 414 us; the launch traced here: 413 us
  waiting for transfers between devices  214 us (52%)
  blocking collectives  75.2 us (18%)
  local copies, waits for them, and re-layouts  36.3 us (9%)
  matrix products  28.4 us (7%)
  other arithmetic  28.1 us (7%)
  starting transfers between devices  16.7 us (4%)
  between operations  14.3 us (3%)
    unnamed x4, waiting for transfers between devices  90.1 us
    psum x5, blocking collectives, by_axis(): return functools.reduce(lax.psum, axes, x)  68.1 us
    all_to_all x2, waiting for transfers between devices, sent_to_all(): lax.all_to_all(jnp.broadcast_to(x[None], (peers, *x.shape)), axis, 0, 0,...  54.7 us
    reduce_scatter x1, waiting for transfers between devices, local(): lax.psum_scatter(lax.dot_general(rows, full_weight, (((1,), (1,)), ((), (...  36.7 us
    all_gather x1, waiting for transfers between devices, local(): full_weight = lax.all_gather(merged_input_weight, DP, axis=0, tiled=True)  32.5 us
    unnamed x66, local copies, waits for them, and re-layouts  24.6 us
    all_to_all x2, starting transfers between devices, sent_to_all(): lax.all_to_all(jnp.broadcast_to(x[None], (peers, *x.shape)), axis, 0, 0,...  16.6 us
    concatenate x1, other arithmetic, local(): jnp.concatenate([lax.dot_general(normed, grad_projected, (((0,), (0,)), (...  9.55 us
  transfers between devices with their start and end apart: 5, of which 4 were waited for; matrix products, arithmetic and copies ran while one was open for 12% of the time, Pallas kernels for 0%

commit v1 on v0

--- a/solution.py
+++ b/solution.py
@@ -126,7 +126,9 @@
     grad_scale = 1.0 / math.sqrt(groups * length)
     local_norm, norm_back = jax.vjp(norm_rows, hidden_in.astype(jnp.float32), norm_gain)
     normed = local_norm.astype(jnp.bfloat16)
-    full_weight = lax.all_gather(merged_input_weight, DP, axis=0, tiled=True)
+    full_weight = jnp.concatenate(
+        lax.all_to_all(jnp.stack([merged_input_weight] * lax.axis_size(DP)), DP, 0, 0), axis=0
+    )
     projected_rows = jnp.dot(normed, full_weight, preferred_element_type=jnp.float32)
     unnormed_query = projected_rows[:, :query_columns].reshape(
         length, key_head_rows, group_width, HEAD_SIZE

time: 414 us -> 517 us (1.25)
  blocking collectives: 75.2 us -> 140 us
  waiting for transfers between devices: 214 us -> 257 us
  starting transfers between devices: 16.7 us -> 10.8 us
    all_to_all x0 -> x1, waiting for transfers between devices: none -> 131 us  [local(): lax.all_to_all(jnp.stack([merged_input_weight] * lax.axis_size(DP)), DP,...]
    all_to_all x1 -> x2, blocking collectives: 7.1 us -> 71.6 us  [sent_to_all(): lax.all_to_all(jnp.broadcast_to(x[None], (peers, *x.shape)), axis, 0, 0,...]
    all_to_all x2 -> x1, waiting for transfers between devices: 54.7 us -> 0.01 us  [sent_to_all(): lax.all_to_all(jnp.broadcast_to(x[None], (peers, *x.shape)), axis, 0, 0,...]
    all_gather x1 -> x0, waiting for transfers between devices: 32.5 us -> none  [local(): full_weight = lax.all_gather(merged_input_weight, DP, axis=0, tiled=True)]
    all_to_all x2 -> x1, starting transfers between devices: 16.6 us -> 5.55 us  [sent_to_all(): lax.all_to_all(jnp.broadcast_to(x[None], (peers, *x.shape)), axis, 0, 0,...]
    unnamed x66 -> x68, local copies, waits for them, and re-layouts: 24.6 us -> 23.6 us
    unnamed x4 -> x3, waiting for transfers between devices: 90.1 us -> 89.4 us
  transfers between devices with their start and end apart: 5 -> 4, of which waited for: 4 -> 3; matrix products, arithmetic and copies ran while one was open for 12% -> 9% of each run, Pallas kernels for 0% -> 0%
where the time goes in v1:
time: 517 us; the launch traced here: 516 us
  waiting for transfers between devices  257 us (50%)
  blocking collectives  140 us (27%)
  local copies, waits for them, and re-layouts  39.8 us (8%)
  matrix products  28.4 us (5%)
  other arithmetic  26.1 us (5%)
  between operations  14.6 us (3%)
  starting transfers between devices  10.8 us (2%)
    all_to_all x1, waiting for transfers between devices, local(): lax.all_to_all(jnp.stack([merged_input_weight] * lax.axis_size(DP)), DP,...  131 us
    unnamed x3, waiting for transfers between devices  89.4 us
    all_to_all x2, blocking collectives, sent_to_all(): lax.all_to_all(jnp.broadcast_to(x[None], (peers, *x.shape)), axis, 0, 0,...  71.6 us
    psum x5, blocking collectives, by_axis(): return functools.reduce(lax.psum, axes, x)  68.1 us
    reduce_scatter x1, waiting for transfers between devices, local(): lax.psum_scatter(lax.dot_general(rows, full_weight, (((1,), (1,)), ((), (...  36 us
    unnamed x68, local copies, waits for them, and re-layouts  23.6 us
  transfers between devices with their start and end apart: 4, of which 3 were waited for; matrix products, arithmetic and copies ran while one was open for 9% of the time, Pallas kernels for 0%

profile of v1, /device:TPU:16, one launch (start us, length us, event | category | flops | bytes accessed | tf_op | source)
XLA Modules:
  0.0 516.1 jit_solution(3768609389358958970)
XLA Ops:
  8.3 63.4 %all_to_all.20 = bf16[16,128,512]{2,1,0:T(8,128)(2,1)S(1)} all-to-all(bf16[16,128,512]{2,1,0:T(8,128)(2,1)S(1)} %broadcast_in_dim.22), channel_id=1, replica_groups=mesh['dp_0'=8,'dp_1'=2,'dp_2'=2,'tensor_0'=4,'tensor_1'=2] {'dp_0','dp_1'}, dimensions={0} | all-to-all | bytes 4194304 | tf_op jit(solution)/shard_map/all_to_all | solution.py:22
  72.2 8.3 %all_to_all.21 = bf16[2,16,128,512]{3,2,1,0:T(8,128)(2,1)} all-to-all(bf16[2,16,128,512]{3,2,1,0:T(8,128)(2,1)S(1)} %broadcast_in_dim.23), channel_id=1, replica_groups=mesh['dp_0'=8,'dp_1'=2,'dp_2'=2,'tensor_0'=4,'tensor_1'=2] {'dp_2'}, dimensions={0} | all-to-all | bytes 8388608 | tf_op jit(solution)/shard_map/all_to_all | solution.py:22
  80.5 3.4 stack.2
  83.9 5.2 all-to-all-start
  91.9 2.8 copy.94
  95.1 2.5 convolution_convert_fusion.2
  97.7 1.9 copy.126
  99.6 131.2 %all-to-all-done = bf16[32,128,768]{2,1,0:T(8,128)(2,1)} async-done(((bf16[32,128,768]{2,1,0:T(8,128)(2,1)}), bf16[32,128,768]{2,1,0:T(8,128)(2,1)}, u32[]{:S(2)}, u32[]{:S(2)}) %all-to-all-start) | async-done | bytes 6291488 | tf_op jit(solution)/shard_map/all_to_all | solution.py:130
  230.8 5.4 %fusion.26 = f32[384,768]{1,0:T(8,128)S(1)} fusion(bf16[4096,768]{1,0:T(8,128)(2,1)} %bitcast, bf16[384,4096]{1,0:T(8,128)(2,1)S(1)} %copy-done, f32[4096]{0:T(1024)S(1)} %copy-done.11, f32[384]{0:T(512)} %add_rsqrt_fusion), kind=kOutput, calls=%fused_computation.40 | convolution fusion | flops 2422210560 | bytes 10634752 | tf_op jit(solution)/shard_map/dot_general | solution.py:132
  254.7 7.1 %convolution_convert_fusion = bf16[384,4096]{1,0:T(8,128)(2,1)} fusion(bf16[4096,768]{1,0:T(8,128)(2,1)} %bitcast, bf16[384,128]{0,1:T(8,128)(2,1)S(1)} %copy-done.30, bf16[384,128]{0,1:T(8,128)(2,1)S(1)} %copy.107, bf16[384,512]{0,1:T(8,128)(2,1)S(1)} %bitcast.136), kind=kOutput, calls=%fused_computation.8 | convolution fusion | flops 2419261440 | bytes 10027008 | tf_op jit(solution)/shard_map/dot_general | solution.py:177
  262.7 1.8 convolution_convert_fusion.1
  264.7 2.3 fusion.3
  267.1 3.9 multiply_convert_fusion
  271.0 9.5 %pad_maximum_fusion = bf16[4096,1280]{0,1:T(8,128)(2,1)} fusion(bf16[4096,512]{0,1:T(8,128)(2,1)S(1)} %fusion.3, bf16[4096,768]{0,1:T(8,128)(2,1)S(1)} %multiply_convert_fusion), kind=kLoop, calls=%fused_computation.1 | loop fusion | flops 20971520 | bytes 20971520 | tf_op jit(solution)/shard_map/concatenate | solution.py:190
  280.5 14.5 %copy.124 = bf16[4096,1280]{1,0:T(8,128)(2,1)} copy(bf16[4096,1280]{0,1:T(8,128)(2,1)} %pad_maximum_fusion) | data formatting | bytes 20971520
  295.2 36.0 %reduce-scatter.5.cloned.1.call-done = bf16[48,4096]{1,0:T(8,128)(2,1)} async-done(((bf16[384,4096]{1,0:T(8,128)(2,1)}), bf16[48,4096]{1,0:T(8,128)(2,1)}) %reduce-scatter.5.cloned.1.call-update) | async-done | bytes 393232 | tf_op jit(solution)/shard_map/reduce_scatter | solution.py:176
  334.1 2.0 broadcast_in_dim.27
  336.1 5.6 %all-to-all-start.3 = ((bf16[8,48,4096]{2,1,0:T(8,128)(2,1)}), bf16[8,48,4096]{2,1,0:T(8,128)(2,1)S(1)}, u32[]{:S(2)}, u32[]{:S(2)}) async-start(bf16[8,48,4096]{2,1,0:T(8,128)(2,1)} %broadcast_in_dim.27), calls=%async_computation.4 | async-start | bytes 6291456 | tf_op jit(solution)/shard_map/all_to_all | solution.py:22
  341.7 30.2 %all-reduce.4 = (f32[4096]{0:T(1024)S(1)}, f32[128]{0:T(128)S(1)}, f32[128]{0:T(128)S(1)}) all-reduce(f32[4096]{0:T(1024)S(1)} %get-tuple-element.36, f32[128]{0:T(128)S(1)} %get-tuple-element.38, f32[128]{0:T(128)S(1)} %get-tuple-element.40), channel_id=1, replica_groups=mesh['dp_0'=8,'dp_1'=2,'dp_2'=2,'tensor_0'=4,'tensor_1'=2] {'dp_0'}, use_global_device_ids=true, to_apply=%region_12.13 | all-reduce | flops 4352 | bytes 34816 | tf_op jit(solution)/shard_map/psum | solution.py:43
  371.9 11.1 %all-reduce.8 = (f32[4096]{0:T(1024)S(1)}, f32[128]{0:T(128)S(1)}, f32[128]{0:T(128)S(1)}) all-reduce(f32[4096]{0:T(1024)S(1)} %get-tuple-element.42, f32[128]{0:T(128)S(1)} %get-tuple-element.43, f32[128]{0:T(128)S(1)} %get-tuple-element.44), channel_id=1, replica_groups=mesh['dp_0'=8,'dp_1'=2,'dp_2'=2,'tensor_0'=4,'tensor_1'=2] {'dp_1'}, use_global_device_ids=true, to_apply=%region_13.14 | all-reduce | flops 4352 | bytes 34816 | tf_op jit(solution)/shard_map/psum | solution.py:43
  383.0 3.4 all-reduce.7
  386.3 15.4 %all-reduce.5 = (f32[4096]{0:T(1024)S(1)}, f32[128]{0:T(128)S(1)}, f32[128]{0:T(128)S(1)}) all-reduce(f32[4096]{0:T(1024)S(1)} %get-tuple-element.51, f32[128]{0:T(128)S(1)} %get-tuple-element.52, f32[128]{0:T(128)S(1)} %get-tuple-element.53), channel_id=1, replica_groups=mesh['dp_0'=8,'dp_1'=2,'dp_2'=2,'tensor_0'=4,'tensor_1'=2] {'tensor_0'}, use_global_device_ids=true, to_apply=%region_15.16 | all-reduce | flops 4352 | bytes 34816 | tf_op jit(solution)/shard_map/psum | solution.py:43
  401.8 8.0 %all-reduce.6 = (f32[4096]{0:T(1024)S(1)}, f32[128]{0:T(128)S(1)}, f32[128]{0:T(128)S(1)}) all-reduce(f32[4096]{0:T(1024)S(1)} %get-tuple-element.45, f32[128]{0:T(128)S(1)} %get-tuple-element.46, f32[128]{0:T(128)S(1)} %get-tuple-element.47), channel_id=1, replica_groups=mesh['dp_0'=8,'dp_1'=2,'dp_2'=2,'tensor_0'=4,'tensor_1'=2] {'tensor_1'}, use_global_device_ids=true, to_apply=%region_16.17 | all-reduce | flops 4352 | bytes 34816 | tf_op jit(solution)/shard_map/psum | solution.py:43
  410.9 89.4 %reduce-scatter.7.cloned.1.call-done = bf16[128,1280]{1,0:T(8,128)(2,1)} async-done(((bf16[4096,1280]{1,0:T(8,128)(2,1)}), bf16[128,1280]{1,0:T(8,128)(2,1)}) %reduce-scatter.7.cloned.1.call-update) | async-done | bytes 327696
  (115 shorter events, 37.2 us)
Async XLA Ops:
  72.2 8.3 %copy-start.10 = (bf16[128,768]{1,0:T(8,128)(2,1)S(1)}, bf16[128,768]{1,0:T(8,128)(2,1)}, u32[]{:S(2)}) copy-start(bf16[128,768]{1,0:T(8,128)(2,1)} %param.9) | copy-start | bytes 589828
  83.9 5.9 %copy-start = (bf16[384,4096]{1,0:T(8,128)(2,1)S(1)}, bf16[384,4096]{1,0:T(8,128)(2,1)}, u32[]{:S(2)}) copy-start(bf16[384,4096]{1,0:T(8,128)(2,1)} %param.7) | copy-start | bytes 9437188
  83.9 146.8 %all-to-all-start = ((bf16[32,128,768]{2,1,0:T(8,128)(2,1)}), bf16[32,128,768]{2,1,0:T(8,128)(2,1)}, u32[]{:S(2)}, u32[]{:S(2)}) async-start(bf16[32,128,768]{2,1,0:T(8,128)(2,1)} %stack.2), calls=%async_computation | async-start | bytes 12582912 | tf_op jit(solution)/shard_map/all_to_all | solution.py:130
  89.1 242.1 %reduce-scatter.5.cloned.1.call-start = ((), (), s32[]{:S(2)}) async-start(), calls=%async_computation.6 | async-start | bytes 3538944 | tf_op jit(solution)/shard_map/reduce_scatter | solution.py:176
  91.9 148.6 %copy-start.3 = (f32[384,64]{1,0:T(8,128)}, f32[384,64]{1,0:T(8,128)S(1)}, u32[]{:S(2)}) copy-start(f32[384,64]{1,0:T(8,128)S(1)} %get-tuple-element.66) | copy-start | bytes 294916
  91.9 3.2 copy-start.14
  95.1 135.6 %copy-start.11 = (f32[4096]{0:T(1024)S(1)}, f32[4096]{0:T(1024)}, u32[]{:S(2)}) copy-start(f32[4096]{0:T(1024)} %param.11) | copy-start | bytes 49156
  236.2 3.1 copy-start.27
  237.2 2.9 copy-start.22
  237.4 3.1 copy-start.18
  238.2 2.6 copy-start.12
  238.3 2.6 copy-start.16
  241.8 3.8 copy-start.20
  248.6 2.7 copy-start.28
  248.6 3.5 copy-start.17
  248.6 3.5 copy-start.25
  248.6 4.7 copy-start.19
  248.7 6.0 %copy-start.30 = (bf16[384,128]{0,1:T(8,128)(2,1)S(1)}, bf16[384,128]{0,1:T(8,128)(2,1)}, u32[]{:S(2)}) copy-start(bf16[384,128]{0,1:T(8,128)(2,1)} %fusion.20) | copy-start | bytes 294916
  251.3 3.3 copy-start.8
  261.8 238.5 %reduce-scatter.7.cloned.1.call-start = ((), (), s32[]{:S(2)}) async-start(), calls=%async_computation.7 | async-start | bytes 10813440
  264.7 2.4 copy-start.1
  264.7 2.4 copy-start.9
  264.7 2.4 copy-start.29
  336.1 74.8 %all-to-all-start.3 = ((bf16[8,48,4096]{2,1,0:T(8,128)(2,1)}), bf16[8,48,4096]{2,1,0:T(8,128)(2,1)S(1)}, u32[]{:S(2)}, u32[]{:S(2)}) async-start(bf16[8,48,4096]{2,1,0:T(8,128)(2,1)} %broadcast_in_dim.27), calls=%async_computation.4 | async-start | bytes 6291456 | tf_op jit(solution)/shard_map/all_to_all | solution.py:22
  (11 other events, 15.1 us)
Sparse Core Ops, SparseCore 0:
  261.9 69.2 reduce-scatter.4
  335.7 164.5 reduce-scatter.6
